TPU v7x, 32 devices: a whole 2x2x4 slice. The times are simulated.
32 devices in a mesh: groups: 2 (over x), box: 16 (over z, y, core).
Axes of the slice: x: 2, y: 2, z: 4, core: 2. Of those that a mesh axis runs over, the one named last changes fastest.
Arguments:
- right_sides: float32 [128, 256, 384], P(('groups', 'box')), parts along dimension 0, may hold values from -6 to 6
- blocks: bfloat16 [128, 4, 4, 256, 256], P(('groups', 'box')), parts along dimension 0, may hold values from -0.1875 to 0.1875
- contrast: float32 [8192], P(('groups', 'box')), parts along dimension 0, may hold values from 0.3 to 3
- sample_index: int32 [64, 256], P('box'), may hold values from 0 to 4095
- owners: int32 [64, 4, 4], P('box'), may hold values from 0 to 3, each once within a row
Outputs:
- scattered: float32 [128, 256, 384], P(('groups', 'box')), parts along dimension 0
There are 2 independent parts, one for each index of `groups`. A program takes and returns all parts, laid end to end along the dimension named above; an argument that names none is the same for every part. Nothing has to cross between parts.
Inputs may be any that keep to these rules, and one draw needn't show every extreme that they name: Each row owners[b, m, :] holds every value 0 to 3 once.
All inputs are finite; a program needn't handle non-finite values.
Results may differ from a plain program's by a relative error of at most 0.0093.
Values may be sent and summed in bfloat16 or wider, within the bound.
No kernel may reach another device: no remote copies, remote signals or barrier semaphores. Data moves between devices by JAX's collectives and lax.ppermute only.
A program may use at most 128 MiB of HBM per device.

v0:
```python
import jax
import jax.numpy as jnp
from jax import lax
from jax.sharding import PartitionSpec as P


def partner(x, axis, distance):
    return lax.ppermute(x, axis, [(i, i ^ 1 << distance) for i in range(lax.axis_size(axis))])


def collect(rounded, first_bit, second_bit):
    position = lax.axis_index("box")
    remote = partner(rounded, "box", first_bit)
    first_value = position >> first_bit & 1
    lower = jnp.where(first_value == 0, rounded, remote)
    upper = jnp.where(first_value == 0, remote, rounded)
    pair_rows = jnp.stack([lower, upper])
    other_pair = partner(pair_rows, "box", second_bit)
    second_value = position >> second_bit & 1
    whole = jnp.where(
        second_value == 0, jnp.stack([pair_rows, other_pair]), jnp.stack([other_pair, pair_rows])
    )
    return whole.reshape((4,) + rounded.shape)


def spread(pieces, first_bit, second_bit):
    position = lax.axis_index("box")
    grid = pieces.reshape((2, 2) + pieces.shape[1:])
    grid = jnp.swapaxes(grid, 0, 1)
    first_value = position >> first_bit & 1
    kept_half = jnp.where(first_value == 0, grid[0], grid[1])
    sent_half = jnp.where(first_value == 0, grid[1], grid[0])
    partial_value = kept_half + partner(sent_half, "box", first_bit)
    second_value = position >> second_bit & 1
    kept_piece = jnp.where(second_value == 0, partial_value[0], partial_value[1])
    sent_piece = jnp.where(second_value == 0, partial_value[1], partial_value[0])
    return kept_piece + partner(sent_piece, "box", second_bit)


def section_bits(layer_index, digit_count):
    low_bit = 2 * ((layer_index - 1) % digit_count)
    high_bit = low_bit + 1
    return (low_bit, high_bit)


def per_device(right_sides, blocks, contrast, sample_index, owners):
    contrast_lookup = lax.all_gather(contrast, "box", axis=0, tiled=True)
    digit_count = (lax.axis_size("box").bit_length() - 1) // 2
    resident_boxes = right_sides.shape[0]
    slots = jnp.arange(4, dtype=jnp.int32)
    current = right_sides
    for layer_index in range(blocks.shape[1]):
        rounded = current.astype(jnp.bfloat16)
        if layer_index == 0:
            gathered_groups = jnp.broadcast_to(rounded[None], (resident_boxes,) + rounded.shape)
        else:
            first_bit, second_bit = section_bits(layer_index, digit_count)
            gathered_groups = jnp.swapaxes(collect(rounded, first_bit, second_bit), 0, 1)
        owner_row = owners[:, layer_index, :]
        inverse = jnp.sum(
            (owner_row[:, :, None] == slots[None, None, :]).astype(jnp.int32)
            * slots[None, :, None],
            axis=1,
        )
        selected_rows = jnp.take_along_axis(gathered_groups, inverse[:, :, None, None], axis=1)
        current = jnp.einsum(
            "pkrs,pksc->prc",
            blocks[:, layer_index],
            selected_rows,
            preferred_element_type=jnp.float32,
        )
    contrast_rows = jnp.take(contrast_lookup, sample_index, axis=0)
    current = current * contrast_rows[:, :, None]
    for layer_index in reversed(range(blocks.shape[1])):
        rounded = current.astype(jnp.bfloat16)
        summand_terms = jnp.einsum(
            "pkrs,prc->pksc", blocks[:, layer_index], rounded, preferred_element_type=jnp.float32
        )
        owner_row = owners[:, layer_index, :]
        positioned_rows = jnp.take_along_axis(summand_terms, owner_row[:, :, None, None], axis=1)
        if layer_index == 0:
            current = jnp.sum(positioned_rows, axis=0)
        else:
            first_bit, second_bit = section_bits(layer_index, digit_count)
            current = spread(jnp.swapaxes(positioned_rows, 0, 1), first_bit, second_bit)
    return current


def solution(mesh):
    return jax.shard_map(
        per_device,
        mesh=mesh,
        in_specs=(
            P(("groups", "box"), None, None),
            P(("groups", "box"), None, None, None, None),
            P(("groups", "box")),
            P("box", None),
            P("box", None, None),
        ),
        out_specs=P(("groups", "box"), None, None),
        check_vma=False,
    )
```

profile of v0, /device:TPU:0, one launch (start us, length us, event | category | flops | bytes accessed | tf_op | source)
XLA Modules:
  0.0 552.1 jit_solution(16012756968478527235)
XLA Ops:
  1.1 1.5 convert_element_type.38
  2.6 2.0 broadcast_in_dim.47
  4.6 3.1 gather_fusion.1
  7.7 2.9 copy.60
  10.6 3.6 fusion.56
  14.8 1.9 collective-permute-done
  16.8 1.3 fusion.98
  18.1 2.9 collective-permute-start.1
  21.2 34.5 %collective-permute-done.1 = bf16[2,4,256,384]{2,3,1,0:T(8,128)(2,1)S(1)} collective-permute-done((bf16[2,4,256,384]{2,3,1,0:T(8,128)(2,1)S(1)}, bf16[2,4,256,384]{2,3,1,0:T(8,128)(2,1)S(1)}, u32[]{:S(2)}, u32[]{:S(2)}) %collective-permute-start.1) | collective-permute-done | bytes 1572896 | tf_op jit(solution)/shard_map/ppermute | solution.py:8
  56.8 3.3 maximum_select_fusion
  60.2 2.4 gather_fusion.2
  62.6 3.6 fusion.61
  66.1 1.9 collective-permute-start.2
  68.0 17.2 %collective-permute-done.2 = bf16[4,256,384]{1,2,0:T(8,128)(2,1)S(1)} collective-permute-done((bf16[4,256,384]{1,2,0:T(8,128)(2,1)S(1)}, bf16[4,256,384]{1,2,0:T(8,128)(2,1)S(1)}, u32[]{:S(2)}, u32[]{:S(2)}) %collective-permute-start.2) | collective-permute-done | bytes 786464 | tf_op jit(solution)/shard_map/ppermute | solution.py:8
  85.3 1.3 fusion.97
  86.7 2.5 collective-permute-start.3
  89.4 66.9 %collective-permute-done.3 = bf16[2,4,256,384]{2,3,1,0:T(8,128)(2,1)S(1)} collective-permute-done((bf16[2,4,256,384]{2,3,1,0:T(8,128)(2,1)S(1)}, bf16[2,4,256,384]{2,3,1,0:T(8,128)(2,1)S(1)}, u32[]{:S(2)}, u32[]{:S(2)}) %collective-permute-start.3) | collective-permute-done | bytes 1572896 | tf_op jit(solution)/shard_map/ppermute | solution.py:8
  157.4 3.3 maximum_select_fusion.1
  160.8 2.4 gather_fusion.3
  163.2 3.6 fusion.66
  166.8 2.3 collective-permute-done.4
  169.2 1.3 fusion.96
  172.2 49.2 %all-gather = f32[16,1,256]{2,1,0:T(1,128)S(1)} all-gather(f32[1,1,256]{2,1,0:T(1,128)S(1)} %bitcast.346), channel_id=1, replica_groups=mesh['groups'=2,'box'=16] {'box'}, dimensions={0}, use_global_device_ids=true | all-gather | bytes 17408 | tf_op jit(solution)/shard_map/all_gather | solution.py:47
  221.4 6.1 %gather_fusion = f32[1024]{0:T(1024)S(1)} fusion(f32[4096]{0:T(1024)S(1)} %bitcast.311, s32[1024]{0:T(1024)S(1)} %broadcast_clamp_fusion), kind=kCustom, calls=%fused_computation.8 | custom fusion | bytes 12288 | tf_op jit(solution)/shard_map/jit(_take)/gather | solution.py:72
  228.8 3.3 maximum_select_fusion.2
  232.1 2.5 gather_fusion.4
  234.6 7.7 %convolution_bitcast_fusion.3 = f32[4,4,256,384]{2,3,1,0:T(8,128)} fusion(bf16[4,4,4,256,256]{4,3,2,1,0:T(8,128)(2,1)} %param.10, bf16[4,4,256,384]{2,3,1,0:T(8,128)(2,1)} %bitcast.327, pred[4,4]{1,0:T(4,128)(4,1)S(1)} %and_bitcast_fusion.4, f32[4,256]{1,0:T(4,128)S(1)} %and_select_fusion), kind=kOutput, calls=%fused_computation.42 | convolution fusion | flops 1612972032 | bytes 13635600 | tf_op jit(solution)/shard_map/pkrs,prc->pksc/dot_general | solution.py:76
  242.3 6.4 %gather_fusion.5 = f32[16,256,384]{1,2,0:T(8,128)} fusion(f32[4,4,256,384]{2,3,1,0:T(8,128)} %convolution_bitcast_fusion.3, s32[16]{0:T(128)S(1)} %reshape.226), kind=kCustom, calls=%fused_computation.1.clone | custom fusion | bytes 12583040 | tf_op jit(solution)/shard_map/jit(take_along_axis)/gather | solution.py:80
  248.6 6.6 %copy.65 = f32[4,4,256,384]{3,2,0,1:T(8,128)} copy(f32[4,4,256,384]{2,3,1,0:T(8,128)} %bitcast.319) | data formatting | bytes 12582912 | tf_op jit(solution)/shard_map/jit(take_along_axis)/gather | solution.py:80
  255.2 3.6 broadcast_select_fusion.2
  259.5 5.3 collective-permute-done.6
  266.8 36.7 %collective-permute-done.7 = f32[4,256,384]{2,1,0:T(8,128)} collective-permute-done((f32[4,256,384]{2,1,0:T(8,128)}, f32[4,256,384]{2,1,0:T(8,128)}, u32[]{:S(2)}, u32[]{:S(2)}) %collective-permute-start.7) | collective-permute-done | bytes 1572896 | tf_op jit(solution)/shard_map/ppermute | solution.py:8
  303.6 5.8 %convolution_bitcast_fusion.2 = f32[4,4,256,384]{2,3,1,0:T(8,128)} fusion(bf16[4,4,4,256,256]{4,3,2,1,0:T(8,128)(2,1)} %param.10, f32[4,256,384]{2,1,0:T(8,128)} %collective-permute-done.7, f32[2,4,256,384]{3,2,1,0:T(8,128)S(1)} %fusion.3, pred[]{:T(512)S(6)} %eq.40), kind=kOutput, calls=%fused_computation.41 | convolution fusion | flops 806486016 | bytes 13107201 | tf_op jit(solution)/shard_map/pkrs,prc->pksc/dot_general | solution.py:76
  309.3 6.4 %gather_fusion.6 = f32[16,256,384]{1,2,0:T(8,128)} fusion(f32[4,4,256,384]{2,3,1,0:T(8,128)} %convolution_bitcast_fusion.2, s32[16]{0:T(128)S(1)} %reshape.231), kind=kCustom, calls=%fused_computation.5.clone | custom fusion | bytes 12583040 | tf_op jit(solution)/shard_map/jit(take_along_axis)/gather | solution.py:80
  315.7 6.6 %copy.71 = f32[4,4,256,384]{3,2,0,1:T(8,128)} copy(f32[4,4,256,384]{2,3,1,0:T(8,128)} %bitcast.320) | data formatting | bytes 12582912 | tf_op jit(solution)/shard_map/jit(take_along_axis)/gather | solution.py:80
  322.3 3.6 broadcast_select_fusion.1
  326.3 69.5 %collective-permute-done.8 = f32[2,4,256,384]{3,2,1,0:T(8,128)S(1)} collective-permute-done((f32[2,4,256,384]{3,2,1,0:T(8,128)S(1)}, f32[2,4,256,384]{3,2,1,0:T(8,128)S(1)}, u32[]{:S(2)}, u32[]{:S(2)}) %collective-permute-start.8) | collective-permute-done | bytes 3145760 | tf_op jit(solution)/shard_map/ppermute | solution.py:8
  397.7 69.6 %collective-permute-done.9 = f32[4,256,384]{2,1,0:T(8,128)} collective-permute-done((f32[4,256,384]{2,1,0:T(8,128)}, f32[4,256,384]{2,1,0:T(8,128)}, u32[]{:S(2)}, u32[]{:S(2)}) %collective-permute-start.9) | collective-permute-done | bytes 1572896 | tf_op jit(solution)/shard_map/ppermute | solution.py:8
  467.4 5.8 %convolution_bitcast_fusion.1 = f32[4,4,256,384]{2,3,1,0:T(8,128)} fusion(bf16[4,4,4,256,256]{4,3,2,1,0:T(8,128)(2,1)} %param.10, f32[4,256,384]{2,1,0:T(8,128)} %collective-permute-done.9, f32[2,4,256,384]{3,2,1,0:T(8,128)S(1)} %fusion.1, pred[]{:T(512)S(6)} %eq.42), kind=kOutput, calls=%fused_computation.40 | convolution fusion | flops 806486016 | bytes 13107201 | tf_op jit(solution)/shard_map/pkrs,prc->pksc/dot_general | solution.py:76
  473.1 6.4 %gather_fusion.7 = f32[16,256,384]{1,2,0:T(8,128)} fusion(f32[4,4,256,384]{2,3,1,0:T(8,128)} %convolution_bitcast_fusion.1, s32[16]{0:T(128)S(1)} %reshape.236), kind=kCustom, calls=%fused_computation.6.clone | custom fusion | bytes 12583040 | tf_op jit(solution)/shard_map/jit(take_along_axis)/gather | solution.py:80
  479.5 6.6 %copy.77 = f32[4,4,256,384]{3,2,0,1:T(8,128)} copy(f32[4,4,256,384]{2,3,1,0:T(8,128)} %bitcast.321) | data formatting | bytes 12582912 | tf_op jit(solution)/shard_map/jit(take_along_axis)/gather | solution.py:80
  486.1 3.6 broadcast_select_fusion
  490.7 5.6 %collective-permute-done.10 = f32[2,4,256,384]{3,2,1,0:T(8,128)S(1)} collective-permute-done((f32[2,4,256,384]{3,2,1,0:T(8,128)S(1)}, f32[2,4,256,384]{3,2,1,0:T(8,128)S(1)}, u32[]{:S(2)}, u32[]{:S(2)}) %collective-permute-start.10) | collective-permute-done | bytes 3145760 | tf_op jit(solution)/shard_map/ppermute | solution.py:8
  499.0 35.8 %collective-permute-done.11 = f32[4,256,384]{2,1,0:T(8,128)} collective-permute-done((f32[4,256,384]{2,1,0:T(8,128)}, f32[4,256,384]{2,1,0:T(8,128)}, u32[]{:S(2)}, u32[]{:S(2)}) %collective-permute-start.11) | collective-permute-done | bytes 1572896 | tf_op jit(solution)/shard_map/ppermute | solution.py:8
  534.8 5.8 %convolution_bitcast_fusion = f32[4,4,256,384]{2,3,1,0:T(8,128)} fusion(bf16[4,4,4,256,256]{4,3,2,1,0:T(8,128)(2,1)} %param.10, f32[4,256,384]{2,1,0:T(8,128)} %collective-permute-done.11, f32[2,4,256,384]{3,2,1,0:T(8,128)S(1)} %bitcast_add_fusion, pred[]{:T(512)S(6)} %eq.40), kind=kOutput, calls=%fused_computation.39 | convolution fusion | flops 806486016 | bytes 13107201 | tf_op jit(solution)/shard_map/pkrs,prc->pksc/dot_general | solution.py:76
  540.6 6.4 %gather_fusion.8 = f32[16,256,384]{1,2,0:T(8,128)} fusion(f32[4,4,256,384]{2,3,1,0:T(8,128)} %convolution_bitcast_fusion, s32[16]{0:T(128)S(1)} %reshape.241), kind=kCustom, calls=%fused_computation.7.clone | custom fusion | bytes 12583040 | tf_op jit(solution)/shard_map/jit(take_along_axis)/gather | solution.py:80
  547.0 3.5 select_reduce_fusion
  550.5 1.6 copy.80
  (70 shorter events, 16.1 us)
Async XLA Ops:
  14.2 2.5 collective-permute-start
  18.1 37.6 %collective-permute-start.1 = (bf16[2,4,256,384]{2,3,1,0:T(8,128)(2,1)S(1)}, bf16[2,4,256,384]{2,3,1,0:T(8,128)(2,1)S(1)}, u32[]{:S(2)}, u32[]{:S(2)}) collective-permute-start(bf16[2,4,256,384]{2,3,1,0:T(8,128)(2,1)S(1)} %get-tuple-element.16), channel_id=1, source_target_pairs={{0,2},{1,3},{2,0},{3,1},{4,6},{5,7},{6,4},{7,5},{8,10},{9,11},{10,... | collective-permute-start | bytes 4718600 | tf_op jit(solution)/shard_map/ppermute | solution.py:8
  55.7 1.1 copy-start.2
  66.1 19.1 %collective-permute-start.2 = (bf16[4,256,384]{1,2,0:T(8,128)(2,1)S(1)}, bf16[4,256,384]{1,2,0:T(8,128)(2,1)S(1)}, u32[]{:S(2)}, u32[]{:S(2)}) collective-permute-start(bf16[4,256,384]{1,2,0:T(8,128)(2,1)S(1)} %fusion.61), channel_id=1, source_target_pairs={{0,4},{1,5},{2,6},{3,7},{4,0},{5,1},{6,2},{7,3},{8,12},{9,13},{10,... | collective-permute-start | bytes 2359304 | tf_op jit(solution)/shard_map/ppermute | solution.py:8
  86.7 69.6 %collective-permute-start.3 = (bf16[2,4,256,384]{2,3,1,0:T(8,128)(2,1)S(1)}, bf16[2,4,256,384]{2,3,1,0:T(8,128)(2,1)S(1)}, u32[]{:S(2)}, u32[]{:S(2)}) collective-permute-start(bf16[2,4,256,384]{2,3,1,0:T(8,128)(2,1)S(1)} %get-tuple-element.12), channel_id=1, source_target_pairs={{0,8},{1,9},{2,10},{3,11},{4,12},{5,13},{6,14},{7,15},{8,0},{9,1},... | collective-permute-start | bytes 4718600 | tf_op jit(solution)/shard_map/ppermute | solution.py:8
  156.3 1.1 copy-start.1
  166.7 2.4 collective-permute-start.4
  169.2 2.6 copy-start.3
  169.2 3.0 copy-start.4
  170.6 57.0 %collective-permute-start.5 = (bf16[2,4,256,384]{2,3,1,0:T(8,128)(2,1)S(1)}, bf16[2,4,256,384]{2,3,1,0:T(8,128)(2,1)S(1)}, u32[]{:S(2)}, u32[]{:S(2)}) collective-permute-start(bf16[2,4,256,384]{2,3,1,0:T(8,128)(2,1)S(1)} %get-tuple-element.8), channel_id=1, source_target_pairs={{0,2},{1,3},{2,0},{3,1},{4,6},{5,7},{6,4},{7,5},{8,10},{9,11},{10,... | collective-permute-start | bytes 4718600 | tf_op jit(solution)/shard_map/ppermute | solution.py:8
  227.6 1.1 copy-start
  259.1 5.7 %collective-permute-start.6 = (f32[2,4,256,384]{3,2,1,0:T(8,128)S(1)}, f32[2,4,256,384]{3,2,1,0:T(8,128)S(1)}, u32[]{:S(2)}, u32[]{:S(2)}) collective-permute-start(f32[2,4,256,384]{3,2,1,0:T(8,128)S(1)} %select_bitcast_fusion.2), channel_id=1, source_target_pairs={{0,1},{1,0},{2,3},{3,2},{4,5},{5,4},{6,7},{7,6},{8,9},{9,8},{10,11... | collective-permute-start | bytes 9437192 | tf_op jit(solution)/shard_map/ppermute | solution.py:8
  266.6 37.0 %collective-permute-start.7 = (f32[4,256,384]{2,1,0:T(8,128)}, f32[4,256,384]{2,1,0:T(8,128)}, u32[]{:S(2)}, u32[]{:S(2)}) collective-permute-start(f32[4,256,384]{2,1,0:T(8,128)} %select_bitcast_fusion.5), channel_id=1, source_target_pairs={{0,2},{1,3},{2,0},{3,1},{4,6},{5,7},{6,4},{7,5},{8,10},{9,11},{10,... | collective-permute-start | bytes 4718600 | tf_op jit(solution)/shard_map/ppermute | solution.py:8
  326.2 69.6 %collective-permute-start.8 = (f32[2,4,256,384]{3,2,1,0:T(8,128)S(1)}, f32[2,4,256,384]{3,2,1,0:T(8,128)S(1)}, u32[]{:S(2)}, u32[]{:S(2)}) collective-permute-start(f32[2,4,256,384]{3,2,1,0:T(8,128)S(1)} %select_bitcast_fusion.1), channel_id=1, source_target_pairs={{0,4},{1,5},{2,6},{3,7},{4,0},{5,1},{6,2},{7,3},{8,12},{9,13},{10,... | collective-permute-start | bytes 9437192 | tf_op jit(solution)/shard_map/ppermute | solution.py:8
  397.5 69.8 %collective-permute-start.9 = (f32[4,256,384]{2,1,0:T(8,128)}, f32[4,256,384]{2,1,0:T(8,128)}, u32[]{:S(2)}, u32[]{:S(2)}) collective-permute-start(f32[4,256,384]{2,1,0:T(8,128)} %select_bitcast_fusion.4), channel_id=1, source_target_pairs={{0,8},{1,9},{2,10},{3,11},{4,12},{5,13},{6,14},{7,15},{8,0},{9,1},... | collective-permute-start | bytes 4718600 | tf_op jit(solution)/shard_map/ppermute | solution.py:8
  490.6 5.7 %collective-permute-start.10 = (f32[2,4,256,384]{3,2,1,0:T(8,128)S(1)}, f32[2,4,256,384]{3,2,1,0:T(8,128)S(1)}, u32[]{:S(2)}, u32[]{:S(2)}) collective-permute-start(f32[2,4,256,384]{3,2,1,0:T(8,128)S(1)} %select_bitcast_fusion), channel_id=1, source_target_pairs={{0,1},{1,0},{2,3},{3,2},{4,5},{5,4},{6,7},{7,6},{8,9},{9,8},{10,11... | collective-permute-start | bytes 9437192 | tf_op jit(solution)/shard_map/ppermute | solution.py:8
  498.1 36.8 %collective-permute-start.11 = (f32[4,256,384]{2,1,0:T(8,128)}, f32[4,256,384]{2,1,0:T(8,128)}, u32[]{:S(2)}, u32[]{:S(2)}) collective-permute-start(f32[4,256,384]{2,1,0:T(8,128)} %select_bitcast_fusion.3), channel_id=1, source_target_pairs={{0,2},{1,3},{2,0},{3,1},{4,6},{5,7},{6,4},{7,5},{8,10},{9,11},{10,... | collective-permute-start | bytes 4718600 | tf_op jit(solution)/shard_map/ppermute | solution.py:8
where the time goes:
time: 553 us; the launch traced here: 552 us
  waiting for transfers between devices  345 us (62%)
  local copies, waits for them, and re-layouts  74.2 us (13%)
  blocking collectives  49.2 us (9%)
  other arithmetic  36.8 us (7%)
  matrix products  35.7 us (6%)
  starting transfers between devices  10.5 us (2%)
    ppermute x12, waiting for transfers between devices, partner(): lax.ppermute(x, axis, [(i, i ^ 1 << distance) for i in range(lax.axis_siz...  345 us
    all_gather x1, blocking collectives, per_device(): contrast_lookup = lax.all_gather(contrast, 'box', axis=0, tiled=True)  49.2 us
    gather x11, local copies, waits for them, and re-layouts, per_device(): jnp.take_along_axis(summand_terms, owner_row[:, :, None, None], axis=1)  45.6 us
    dot_general x4, matrix products, per_device(): jnp.einsum('pkrs,prc->pksc', blocks[:, layer_index], rounded, preferred_e...  25 us
    gather x9, local copies, waits for them, and re-layouts, per_device(): jnp.take_along_axis(gathered_groups, inverse[:, :, None, None], axis=1)  13.6 us
  transfers between devices with their start and end apart: 12, of which 11 were waited for; matrix products, arithmetic and copies ran while one was open for 1% of the time, Pallas kernels for 0%

commit v1 on v0

--- a/solution.py
+++ b/solution.py
@@ -44,7 +44,8 @@
 
 
 def per_device(right_sides, blocks, contrast, sample_index, owners):
-    contrast_lookup = lax.all_gather(contrast, "box", axis=0, tiled=True)
+    repeated = jnp.stack([contrast] * lax.axis_size("box"))
+    contrast_lookup = jnp.concatenate(lax.all_to_all(repeated, "box", 0, 0), axis=0)
     digit_count = (lax.axis_size("box").bit_length() - 1) // 2
     resident_boxes = right_sides.shape[0]
     slots = jnp.arange(4, dtype=jnp.int32)

time: 553 us -> 536 us (0.969)
  blocking collectives: 49.2 us -> 0 us
  waiting for transfers between devices: 345 us -> 365 us
  starting transfers between devices: 10.5 us -> 22.7 us
    all_gather x1 -> x0, blocking collectives: 49.2 us -> none  [per_device(): contrast_lookup = lax.all_gather(contrast, 'box', axis=0, tiled=True)]
    ppermute x12, waiting for transfers between devices: 345 us -> 362 us  [partner(): lax.ppermute(x, axis, [(i, i ^ 1 << distance) for i in range(lax.axis_siz...]
    ppermute x12, starting transfers between devices: 10.5 us -> 17.2 us  [partner(): lax.ppermute(x, axis, [(i, i ^ 1 << distance) for i in range(lax.axis_siz...]
    all_to_all x0 -> x1, starting transfers between devices: none -> 5.59 us  [per_device(): lax.all_to_all(repeated, 'box', 0, 0)]
  transfers between devices with their start and end apart: 12 -> 13, of which waited for: 11 -> 12; matrix products, arithmetic and copies ran while one was open for 1% -> 2% of each run, Pallas kernels for 0% -> 0%
where the time goes in v1:
time: 536 us; the launch traced here: 535 us
  waiting for transfers between devices  365 us (68%)
  local copies, waits for them, and re-layouts  74.9 us (14%)
  other arithmetic  36.9 us (7%)
  matrix products  35.7 us (7%)
  starting transfers between devices  22.7 us (4%)
    ppermute x12, waiting for transfers between devices, partner(): lax.ppermute(x, axis, [(i, i ^ 1 << distance) for i in range(lax.axis_siz...  362 us
    gather x11, local copies, waits for them, and re-layouts, per_device(): jnp.take_along_axis(summand_terms, owner_row[:, :, None, None], axis=1)  45.6 us
    dot_general x4, matrix products, per_device(): jnp.einsum('pkrs,prc->pksc', blocks[:, layer_index], rounded, preferred_e...  25 us
    ppermute x12, starting transfers between devices, partner(): lax.ppermute(x, axis, [(i, i ^ 1 << distance) for i in range(lax.axis_siz...  17.2 us
    gather x9, local copies, waits for them, and re-layouts, per_device(): jnp.take_along_axis(gathered_groups, inverse[:, :, None, None], axis=1)  13.6 us
  transfers between devices with their start and end apart: 13, of which 12 were waited for; matrix products, arithmetic and copies ran while one was open for 2% of the time, Pallas kernels for 0%

profile of v1, /device:TPU:0, one launch (start us, length us, event | category | flops | bytes accessed | tf_op | source)
XLA Modules:
  0.0 535.4 jit_solution(12141529278424429905)
XLA Ops:
  2.6 2.0 broadcast_in_dim.47
  4.6 3.1 gather_fusion.1
  7.7 2.9 copy.60
  10.6 3.6 fusion.56
  14.7 1.9 collective-permute-done
  18.1 2.9 collective-permute-start.1
  21.2 34.5 %collective-permute-done.1 = bf16[2,4,256,384]{2,3,1,0:T(8,128)(2,1)S(1)} collective-permute-done((bf16[2,4,256,384]{2,3,1,0:T(8,128)(2,1)S(1)}, bf16[2,4,256,384]{2,3,1,0:T(8,128)(2,1)S(1)}, u32[]{:S(2)}, u32[]{:S(2)}) %collective-permute-start.1) | collective-permute-done | bytes 1572896 | tf_op jit(solution)/shard_map/ppermute | solution.py:8
  56.8 3.4 maximum_select_fusion
  60.2 2.4 gather_fusion.2
  62.6 3.6 fusion.61
  66.2 1.9 collective-permute-start.2
  68.1 17.2 %collective-permute-done.2 = bf16[4,256,384]{1,2,0:T(8,128)(2,1)S(1)} collective-permute-done((bf16[4,256,384]{1,2,0:T(8,128)(2,1)S(1)}, bf16[4,256,384]{1,2,0:T(8,128)(2,1)S(1)}, u32[]{:S(2)}, u32[]{:S(2)}) %collective-permute-start.2) | collective-permute-done | bytes 786464 | tf_op jit(solution)/shard_map/ppermute | solution.py:8
  86.7 2.5 collective-permute-start.3
  89.4 66.9 %collective-permute-done.3 = bf16[2,4,256,384]{2,3,1,0:T(8,128)(2,1)S(1)} collective-permute-done((bf16[2,4,256,384]{2,3,1,0:T(8,128)(2,1)S(1)}, bf16[2,4,256,384]{2,3,1,0:T(8,128)(2,1)S(1)}, u32[]{:S(2)}, u32[]{:S(2)}) %collective-permute-start.3) | collective-permute-done | bytes 1572896 | tf_op jit(solution)/shard_map/ppermute | solution.py:8
  157.5 3.4 maximum_select_fusion.1
  160.9 2.4 gather_fusion.3
  163.3 3.6 fusion.66
  167.5 5.6 %all-to-all-start = ((f32[16,1,256]{2,1,0:T(1,128)}), f32[16,1,256]{2,1,0:T(1,128)S(1)}, u32[]{:S(2)}, u32[]{:S(2)}) async-start(f32[16,1,256]{2,1,0:T(1,128)} %stack.109), calls=%async_computation | async-start | bytes 32768 | tf_op jit(solution)/shard_map/all_to_all | solution.py:48
  174.6 1.9 collective-permute-start.5
  177.0 2.7 all-to-all-done
  179.7 6.1 %gather_fusion = f32[1024]{0:T(1024)S(1)} fusion(f32[4096]{0:T(1024)S(1)} %bitcast.310, s32[1024]{0:T(1024)S(1)} %broadcast_clamp_fusion), kind=kCustom, calls=%fused_computation.8 | custom fusion | bytes 12288 | tf_op jit(solution)/shard_map/jit(_take)/gather | solution.py:73
  185.9 25.6 %collective-permute-done.5 = bf16[2,4,256,384]{2,3,1,0:T(8,128)(2,1)S(1)} collective-permute-done((bf16[2,4,256,384]{2,3,1,0:T(8,128)(2,1)S(1)}, bf16[2,4,256,384]{2,3,1,0:T(8,128)(2,1)S(1)}, u32[]{:S(2)}, u32[]{:S(2)}) %collective-permute-start.5) | collective-permute-done | bytes 1572896 | tf_op jit(solution)/shard_map/ppermute | solution.py:8
  212.6 3.4 maximum_select_fusion.2
  216.0 2.5 gather_fusion.4
  218.4 7.7 %convolution_bitcast_fusion.3 = f32[4,4,256,384]{2,3,1,0:T(8,128)} fusion(bf16[4,4,4,256,256]{4,3,2,1,0:T(8,128)(2,1)} %param.10, bf16[4,4,256,384]{2,3,1,0:T(8,128)(2,1)} %bitcast.326, pred[4,4]{1,0:T(4,128)(4,1)S(1)} %and_bitcast_fusion.4, f32[4,256]{1,0:T(4,128)S(1)} %and_select_fusion), kind=kOutput, calls=%fused_computation.42 | convolution fusion | flops 1612972032 | bytes 13635600 | tf_op jit(solution)/shard_map/pkrs,prc->pksc/dot_general | solution.py:77
  226.1 6.4 %gather_fusion.5 = f32[16,256,384]{1,2,0:T(8,128)} fusion(f32[4,4,256,384]{2,3,1,0:T(8,128)} %convolution_bitcast_fusion.3, s32[16]{0:T(128)S(1)} %reshape.236), kind=kCustom, calls=%fused_computation.1.clone | custom fusion | bytes 12583040 | tf_op jit(solution)/shard_map/jit(take_along_axis)/gather | solution.py:81
  232.5 6.6 %copy.65 = f32[4,4,256,384]{3,2,0,1:T(8,128)} copy(f32[4,4,256,384]{2,3,1,0:T(8,128)} %bitcast.318) | data formatting | bytes 12582912 | tf_op jit(solution)/shard_map/jit(take_along_axis)/gather | solution.py:81
  239.1 3.6 broadcast_select_fusion.2
  243.1 5.6 %collective-permute-done.6 = f32[2,4,256,384]{3,2,1,0:T(8,128)S(1)} collective-permute-done((f32[2,4,256,384]{3,2,1,0:T(8,128)S(1)}, f32[2,4,256,384]{3,2,1,0:T(8,128)S(1)}, u32[]{:S(2)}, u32[]{:S(2)}) %collective-permute-start.6) | collective-permute-done | bytes 3145760 | tf_op jit(solution)/shard_map/ppermute | solution.py:8
  252.2 35.0 %collective-permute-done.7 = f32[4,256,384]{2,1,0:T(8,128)} collective-permute-done((f32[4,256,384]{2,1,0:T(8,128)}, f32[4,256,384]{2,1,0:T(8,128)}, u32[]{:S(2)}, u32[]{:S(2)}) %collective-permute-start.7) | collective-permute-done | bytes 1572896 | tf_op jit(solution)/shard_map/ppermute | solution.py:8
  287.2 5.8 %convolution_bitcast_fusion.2 = f32[4,4,256,384]{2,3,1,0:T(8,128)} fusion(bf16[4,4,4,256,256]{4,3,2,1,0:T(8,128)(2,1)} %param.10, f32[4,256,384]{2,1,0:T(8,128)} %collective-permute-done.7, f32[2,4,256,384]{3,2,1,0:T(8,128)S(1)} %fusion.3, pred[]{:T(512)S(6)} %eq.40), kind=kOutput, calls=%fused_computation.41 | convolution fusion | flops 806486016 | bytes 13107201 | tf_op jit(solution)/shard_map/pkrs,prc->pksc/dot_general | solution.py:77
  293.0 6.4 %gather_fusion.6 = f32[16,256,384]{1,2,0:T(8,128)} fusion(f32[4,4,256,384]{2,3,1,0:T(8,128)} %convolution_bitcast_fusion.2, s32[16]{0:T(128)S(1)} %reshape.241), kind=kCustom, calls=%fused_computation.5.clone | custom fusion | bytes 12583040 | tf_op jit(solution)/shard_map/jit(take_along_axis)/gather | solution.py:81
  299.4 6.6 %copy.71 = f32[4,4,256,384]{3,2,0,1:T(8,128)} copy(f32[4,4,256,384]{2,3,1,0:T(8,128)} %bitcast.319) | data formatting | bytes 12582912 | tf_op jit(solution)/shard_map/jit(take_along_axis)/gather | solution.py:81
  306.0 3.6 broadcast_select_fusion.1
  309.8 1.6 collective-permute-start.8
  311.5 67.7 %collective-permute-done.8 = f32[2,4,256,384]{3,2,1,0:T(8,128)S(1)} collective-permute-done((f32[2,4,256,384]{3,2,1,0:T(8,128)S(1)}, f32[2,4,256,384]{3,2,1,0:T(8,128)S(1)}, u32[]{:S(2)}, u32[]{:S(2)}) %collective-permute-start.8) | collective-permute-done | bytes 3145760 | tf_op jit(solution)/shard_map/ppermute | solution.py:8
  381.0 2.4 collective-permute-start.9
  383.6 67.0 %collective-permute-done.9 = f32[4,256,384]{2,1,0:T(8,128)} collective-permute-done((f32[4,256,384]{2,1,0:T(8,128)}, f32[4,256,384]{2,1,0:T(8,128)}, u32[]{:S(2)}, u32[]{:S(2)}) %collective-permute-start.9) | collective-permute-done | bytes 1572896 | tf_op jit(solution)/shard_map/ppermute | solution.py:8
  450.6 5.8 %convolution_bitcast_fusion.1 = f32[4,4,256,384]{2,3,1,0:T(8,128)} fusion(bf16[4,4,4,256,256]{4,3,2,1,0:T(8,128)(2,1)} %param.10, f32[4,256,384]{2,1,0:T(8,128)} %collective-permute-done.9, f32[2,4,256,384]{3,2,1,0:T(8,128)S(1)} %fusion.1, pred[]{:T(512)S(6)} %eq.42), kind=kOutput, calls=%fused_computation.40 | convolution fusion | flops 806486016 | bytes 13107201 | tf_op jit(solution)/shard_map/pkrs,prc->pksc/dot_general | solution.py:77
  456.4 6.4 %gather_fusion.7 = f32[16,256,384]{1,2,0:T(8,128)} fusion(f32[4,4,256,384]{2,3,1,0:T(8,128)} %convolution_bitcast_fusion.1, s32[16]{0:T(128)S(1)} %reshape.246), kind=kCustom, calls=%fused_computation.6.clone | custom fusion | bytes 12583040 | tf_op jit(solution)/shard_map/jit(take_along_axis)/gather | solution.py:81
  462.8 6.6 %copy.77 = f32[4,4,256,384]{3,2,0,1:T(8,128)} copy(f32[4,4,256,384]{2,3,1,0:T(8,128)} %bitcast.320) | data formatting | bytes 12582912 | tf_op jit(solution)/shard_map/jit(take_along_axis)/gather | solution.py:81
  469.3 3.6 broadcast_select_fusion
  473.9 5.6 %collective-permute-done.10 = f32[2,4,256,384]{3,2,1,0:T(8,128)S(1)} collective-permute-done((f32[2,4,256,384]{3,2,1,0:T(8,128)S(1)}, f32[2,4,256,384]{3,2,1,0:T(8,128)S(1)}, u32[]{:S(2)}, u32[]{:S(2)}) %collective-permute-start.10) | collective-permute-done | bytes 3145760 | tf_op jit(solution)/shard_map/ppermute | solution.py:8
  483.0 35.1 %collective-permute-done.11 = f32[4,256,384]{2,1,0:T(8,128)} collective-permute-done((f32[4,256,384]{2,1,0:T(8,128)}, f32[4,256,384]{2,1,0:T(8,128)}, u32[]{:S(2)}, u32[]{:S(2)}) %collective-permute-start.11) | collective-permute-done | bytes 1572896 | tf_op jit(solution)/shard_map/ppermute | solution.py:8
  518.0 5.8 %convolution_bitcast_fusion = f32[4,4,256,384]{2,3,1,0:T(8,128)} fusion(bf16[4,4,4,256,256]{4,3,2,1,0:T(8,128)(2,1)} %param.10, f32[4,256,384]{2,1,0:T(8,128)} %collective-permute-done.11, f32[2,4,256,384]{3,2,1,0:T(8,128)S(1)} %bitcast_add_fusion, pred[]{:T(512)S(6)} %eq.40), kind=kOutput, calls=%fused_computation.39 | convolution fusion | flops 806486016 | bytes 13107201 | tf_op jit(solution)/shard_map/pkrs,prc->pksc/dot_general | solution.py:77
  523.8 6.4 %gather_fusion.8 = f32[16,256,384]{1,2,0:T(8,128)} fusion(f32[4,4,256,384]{2,3,1,0:T(8,128)} %convolution_bitcast_fusion, s32[16]{0:T(128)S(1)} %reshape.251), kind=kCustom, calls=%fused_computation.7.clone | custom fusion | bytes 12583040 | tf_op jit(solution)/shard_map/jit(take_along_axis)/gather | solution.py:81
  530.2 3.5 select_reduce_fusion
  533.7 1.6 copy.80
  (72 shorter events, 23.0 us)
Async XLA Ops:
  14.2 2.5 collective-permute-start
  18.1 37.6 %collective-permute-start.1 = (bf16[2,4,256,384]{2,3,1,0:T(8,128)(2,1)S(1)}, bf16[2,4,256,384]{2,3,1,0:T(8,128)(2,1)S(1)}, u32[]{:S(2)}, u32[]{:S(2)}) collective-permute-start(bf16[2,4,256,384]{2,3,1,0:T(8,128)(2,1)S(1)} %get-tuple-element.16), channel_id=1, source_target_pairs={{0,2},{1,3},{2,0},{3,1},{4,6},{5,7},{6,4},{7,5},{8,10},{9,11},{10,... | collective-permute-start | bytes 4718600 | tf_op jit(solution)/shard_map/ppermute | solution.py:8
  55.7 1.2 copy-start.2
  66.2 19.1 %collective-permute-start.2 = (bf16[4,256,384]{1,2,0:T(8,128)(2,1)S(1)}, bf16[4,256,384]{1,2,0:T(8,128)(2,1)S(1)}, u32[]{:S(2)}, u32[]{:S(2)}) collective-permute-start(bf16[4,256,384]{1,2,0:T(8,128)(2,1)S(1)} %fusion.61), channel_id=1, source_target_pairs={{0,4},{1,5},{2,6},{3,7},{4,0},{5,1},{6,2},{7,3},{8,12},{9,13},{10,... | collective-permute-start | bytes 2359304 | tf_op jit(solution)/shard_map/ppermute | solution.py:8
  86.7 69.6 %collective-permute-start.3 = (bf16[2,4,256,384]{2,3,1,0:T(8,128)(2,1)S(1)}, bf16[2,4,256,384]{2,3,1,0:T(8,128)(2,1)S(1)}, u32[]{:S(2)}, u32[]{:S(2)}) collective-permute-start(bf16[2,4,256,384]{2,3,1,0:T(8,128)(2,1)S(1)} %get-tuple-element.12), channel_id=1, source_target_pairs={{0,8},{1,9},{2,10},{3,11},{4,12},{5,13},{6,14},{7,15},{8,0},{9,1},... | collective-permute-start | bytes 4718600 | tf_op jit(solution)/shard_map/ppermute | solution.py:8
  156.3 1.2 copy-start.1
  163.3 3.7 copy-start.4
  166.8 6.3 %collective-permute-start.4 = (bf16[4,256,384]{1,2,0:T(8,128)(2,1)S(1)}, bf16[4,256,384]{1,2,0:T(8,128)(2,1)S(1)}, u32[]{:S(2)}, u32[]{:S(2)}) collective-permute-start(bf16[4,256,384]{1,2,0:T(8,128)(2,1)S(1)} %fusion.66), channel_id=1, source_target_pairs={{0,1},{1,0},{2,3},{3,2},{4,5},{5,4},{6,7},{7,6},{8,9},{9,8},{10,11... | collective-permute-start | bytes 2359304 | tf_op jit(solution)/shard_map/ppermute | solution.py:8
  167.5 12.1 %all-to-all-start = ((f32[16,1,256]{2,1,0:T(1,128)}), f32[16,1,256]{2,1,0:T(1,128)S(1)}, u32[]{:S(2)}, u32[]{:S(2)}) async-start(f32[16,1,256]{2,1,0:T(1,128)} %stack.109), calls=%async_computation | async-start | bytes 32768 | tf_op jit(solution)/shard_map/all_to_all | solution.py:48
  173.3 3.3 copy-start.3
  174.6 36.8 %collective-permute-start.5 = (bf16[2,4,256,384]{2,3,1,0:T(8,128)(2,1)S(1)}, bf16[2,4,256,384]{2,3,1,0:T(8,128)(2,1)S(1)}, u32[]{:S(2)}, u32[]{:S(2)}) collective-permute-start(bf16[2,4,256,384]{2,3,1,0:T(8,128)(2,1)S(1)} %get-tuple-element.8), channel_id=1, source_target_pairs={{0,2},{1,3},{2,0},{3,1},{4,6},{5,7},{6,4},{7,5},{8,10},{9,11},{10,... | collective-permute-start | bytes 4718600 | tf_op jit(solution)/shard_map/ppermute | solution.py:8
  211.4 1.2 copy-start
  243.0 5.7 %collective-permute-start.6 = (f32[2,4,256,384]{3,2,1,0:T(8,128)S(1)}, f32[2,4,256,384]{3,2,1,0:T(8,128)S(1)}, u32[]{:S(2)}, u32[]{:S(2)}) collective-permute-start(f32[2,4,256,384]{3,2,1,0:T(8,128)S(1)} %select_bitcast_fusion.2), channel_id=1, source_target_pairs={{0,1},{1,0},{2,3},{3,2},{4,5},{5,4},{6,7},{7,6},{8,9},{9,8},{10,11... | collective-permute-start | bytes 9437192 | tf_op jit(solution)/shard_map/ppermute | solution.py:8
  250.5 36.8 %collective-permute-start.7 = (f32[4,256,384]{2,1,0:T(8,128)}, f32[4,256,384]{2,1,0:T(8,128)}, u32[]{:S(2)}, u32[]{:S(2)}) collective-permute-start(f32[4,256,384]{2,1,0:T(8,128)} %select_bitcast_fusion.5), channel_id=1, source_target_pairs={{0,2},{1,3},{2,0},{3,1},{4,6},{5,7},{6,4},{7,5},{8,10},{9,11},{10,... | collective-permute-start | bytes 4718600 | tf_op jit(solution)/shard_map/ppermute | solution.py:8
  309.8 69.4 %collective-permute-start.8 = (f32[2,4,256,384]{3,2,1,0:T(8,128)S(1)}, f32[2,4,256,384]{3,2,1,0:T(8,128)S(1)}, u32[]{:S(2)}, u32[]{:S(2)}) collective-permute-start(f32[2,4,256,384]{3,2,1,0:T(8,128)S(1)} %select_bitcast_fusion.1), channel_id=1, source_target_pairs={{0,4},{1,5},{2,6},{3,7},{4,0},{5,1},{6,2},{7,3},{8,12},{9,13},{10,... | collective-permute-start | bytes 9437192 | tf_op jit(solution)/shard_map/ppermute | solution.py:8
  381.0 69.6 %collective-permute-start.9 = (f32[4,256,384]{2,1,0:T(8,128)}, f32[4,256,384]{2,1,0:T(8,128)}, u32[]{:S(2)}, u32[]{:S(2)}) collective-permute-start(f32[4,256,384]{2,1,0:T(8,128)} %select_bitcast_fusion.4), channel_id=1, source_target_pairs={{0,8},{1,9},{2,10},{3,11},{4,12},{5,13},{6,14},{7,15},{8,0},{9,1},... | collective-permute-start | bytes 4718600 | tf_op jit(solution)/shard_map/ppermute | solution.py:8
  473.8 5.7 %collective-permute-start.10 = (f32[2,4,256,384]{3,2,1,0:T(8,128)S(1)}, f32[2,4,256,384]{3,2,1,0:T(8,128)S(1)}, u32[]{:S(2)}, u32[]{:S(2)}) collective-permute-start(f32[2,4,256,384]{3,2,1,0:T(8,128)S(1)} %select_bitcast_fusion), channel_id=1, source_target_pairs={{0,1},{1,0},{2,3},{3,2},{4,5},{5,4},{6,7},{7,6},{8,9},{9,8},{10,11... | collective-permute-start | bytes 9437192 | tf_op jit(solution)/shard_map/ppermute | solution.py:8
  481.3 36.8 %collective-permute-start.11 = (f32[4,256,384]{2,1,0:T(8,128)}, f32[4,256,384]{2,1,0:T(8,128)}, u32[]{:S(2)}, u32[]{:S(2)}) collective-permute-start(f32[4,256,384]{2,1,0:T(8,128)} %select_bitcast_fusion.3), channel_id=1, source_target_pairs={{0,2},{1,3},{2,0},{3,1},{4,6},{5,7},{6,4},{7,5},{8,10},{9,11},{10,... | collective-permute-start | bytes 4718600 | tf_op jit(solution)/shard_map/ppermute | solution.py:8
